TPU v7x, 32 devices: a whole 2x2x4 slice. The times are simulated.
32 devices in a mesh: pole: 4 (over x, core), row: 4 (over z), col: 2 (over y).
Axes of the slice: x: 2, y: 2, z: 4, core: 2. Of those that a mesh axis runs over, the one named last changes fastest.
Arguments:
- anc_inverse: bfloat16 [4, 2, 4, 192, 768], P('pole', None, None, 'col', 'row'), may hold values from -6 to 6
- panel: bfloat16 [4, 2, 768, 1024], P('pole', None, ('row', 'col')), may hold values from -0.21875 to 0.21875
- pattern: int32 [8, 2], replicated, may hold values 0 or 1
- diag_inverse: bfloat16 [4, 2, 1024, 512], P('pole', None, 'col', 'row'), may hold values from -6 to 6
- pole_weights: float32 [4, 2], P('pole'), may hold values from -4 to 4
Outputs:
- inv_panel: float32 [4, 2, 768, 1024], P('pole', None, 'row', 'col')
- inv_diag: bfloat16 [4, 2, 1024, 512], P('pole', None, 'col', 'row')
- density: float32 [1024, 512], P('col', 'row')
All inputs are finite; a program needn't handle non-finite values.
Results may differ from a plain program's by a relative error of at most 0.013.
Values may be sent and summed in bfloat16 or wider, within the bound.
A program may use at most 128 MiB of HBM per device.

v0:
```python
import jax
import jax.numpy as jnp
from jax import lax
from jax.sharding import PartitionSpec as P


def complex_left(left_re, left_im, right_re, right_im):
    upper = jnp.concatenate([left_re, left_im], axis=1)
    lower = jnp.concatenate([-left_im, left_re], axis=1)
    left_side = jnp.concatenate([upper, lower], axis=0)
    right_side = jnp.concatenate([right_re, right_im], axis=0)
    product = lax.dot_general(
        left_side, right_side, (((0,), (0,)), ((), ())), preferred_element_type=jnp.float32
    )
    return product.reshape(2, left_re.shape[1], right_re.shape[1])


def body(anc_inverse, panel, pattern, diag_inverse, pole_weights):
    n_row = lax.axis_size("row")
    n_col = lax.axis_size("col")
    fine_block = lax.axis_index("row") * n_col + lax.axis_index("col")
    pattern_row = lax.dynamic_slice_in_dim(pattern, fine_block, 1, 0)
    block_rows = panel.shape[2]
    width_all = panel.shape[3]
    groups = pattern.shape[1]
    keep_mask = pattern_row.astype(jnp.bfloat16).reshape(1, 1, 1, groups, 1)
    masked = (panel.reshape(1, 2, block_rows, groups, width_all // groups) * keep_mask).reshape(
        1, 2, block_rows, width_all
    )
    local_rows = lax.all_to_all(masked, "col", split_axis=3, concat_axis=2, tiled=True)
    row_count = anc_inverse.shape[4]
    col_count = local_rows.shape[3]
    full_cols = lax.all_gather(local_rows, "row", axis=2, tiled=True)
    stacked = full_cols[0].reshape(2, n_row, block_rows * n_col, col_count)
    segment = lax.all_gather(anc_inverse, "col", axis=3, tiled=True)
    length = segment.shape[3]
    left_side = segment[0].reshape(2, n_row * length, row_count)
    right_side = stacked.reshape(2, n_row * length, col_count)
    summed = complex_left(left_side[0], left_side[1], right_side[0], right_side[1])
    result_panel = -summed
    rounded = result_panel.astype(jnp.bfloat16)
    diag_terms = complex_left(local_rows[0, 0], local_rows[0, 1], rounded[0], rounded[1])
    row_share = lax.psum_scatter(diag_terms, "row", scatter_dimension=2, tiled=True)
    inverse_diag = diag_inverse[0].astype(jnp.float32) - row_share
    pole_weight = pole_weights[0]
    density_term = pole_weight[0] * inverse_diag[1] + pole_weight[1] * inverse_diag[0]
    density = lax.psum(density_term.astype(jnp.bfloat16), "pole").astype(jnp.float32)
    return (result_panel[None], inverse_diag.astype(jnp.bfloat16)[None], density)


def solution(mesh):
    placed = (
        P("pole", None, None, "col", "row"),
        P("pole", None, ("row", "col"), None),
        P(),
        P("pole", None, "col", "row"),
        P("pole", None),
    )
    return jax.shard_map(
        body,
        mesh=mesh,
        in_specs=placed,
        out_specs=(P("pole", None, "row", "col"), P("pole", None, "col", "row"), P("col", "row")),
        check_vma=False,
    )
```

profile of v0, /device:TPU:0, one launch (start us, length us, event | category | flops | bytes accessed | tf_op | source)
XLA Modules:
  0.0 151.4 jit_solution(4732061525736366362)
XLA Ops:
  7.2 0.0 all-gather.2.cloned.1.call-start
  7.2 0.9 fusion.26
  8.1 0.1 broadcast_bitcast_fusion
  8.2 1.0 broadcast_multiply_fusion
  9.2 0.4 copy.12
  9.6 0.0 copy-start.1
  9.6 12.2 %all_to_all.18 = bf16[1,2,96,1024]{2,1,0,3:T(2,128)(2,1)S(1)} all-to-all(bf16[1,2,96,1024]{2,1,0,3:T(2,128)(2,1)S(1)} %copy.12), channel_id=1, replica_groups=mesh['pole'=4,'row'=4,'col'=2] {'col'}, dimensions={3} | all-to-all | bytes 786432 | tf_op jit(solution)/shard_map/all_to_all | solution.py:30
  21.8 0.8 copy.15
  22.6 0.8 copy.14
  23.4 0.0 all-gather.2.cloned.1.call-update
  23.4 0.0 copy-start
  23.4 0.0 reduce-scatter.2.cloned.1.call-start
  23.5 0.0 copy-done.1
  23.5 10.5 %all_gather.6 = bf16[1,2,4,192,192]{4,3,2,1,0:T(8,128)(2,1)S(1)} all-gather(bf16[1,2,4,96,192]{4,3,2,1,0:T(8,128)(2,1)S(1)} %copy-done.1), channel_id=1, replica_groups=mesh['pole'=4,'row'=4,'col'=2] {'col'}, dimensions={3}, use_global_device_ids=true | all-gather | bytes 884736 | tf_op jit(solution)/shard_map/all_gather | solution.py:35
  34.0 0.1 fusion.30
  34.1 0.1 bitcast_negate_fusion
  34.1 0.0 copy-done
  34.2 26.8 %all-gather.2.cloned.1.call-done = bf16[1,2,768,512]{3,2,1,0:T(8,128)(2,1)} async-done(((bf16[1,2,192,512]{3,2,1,0:T(8,128)(2,1)}), bf16[1,2,768,512]{3,2,1,0:T(8,128)(2,1)}) %all-gather.2.cloned.1.call-update) | async-done | bytes 1572880 | tf_op jit(solution)/shard_map/all_gather | solution.py:33
  61.0 1.5 slice_bitcast_fusion.1
  62.5 1.1 fusion.4
  63.6 0.0 copy-start.4
  63.6 2.1 %fusion.14 = f32[1024,512]{1,0:T(8,128)} fusion(bf16[192,512]{1,0:T(8,128)(2,1)S(1)} %get-tuple-element.10, bf16[192,512]{1,0:T(8,128)(2,1)S(1)} %fusion.29, bf16[192,512]{1,0:T(8,128)(2,1)S(1)} %get-tuple-element.9, f32[384,512]{1,0:T(8,128)S(1)} %fusion.4), kind=kOutput, calls=%fused_computation.14 | convolution fusion | flops 405995520 | bytes 3473408 | tf_op jit(solution)/shard_map/dot_general | solution.py:12
  65.7 0.0 reduce-scatter.2.cloned.1.call-update
  65.7 0.0 all-reduce.2.cloned.1.call-start
  65.8 0.6 copy-done.3
  66.3 0.6 fusion.31
  67.0 41.4 %reduce-scatter.2.cloned.1.call-done = f32[2,512,128]{2,1,0:T(8,128)} async-done(((f32[2,512,512]{2,1,0:T(8,128)}), f32[2,512,128]{2,1,0:T(8,128)}) %reduce-scatter.2.cloned.1.call-update) | async-done | bytes 524304 | tf_op jit(solution)/shard_map/reduce_scatter | solution.py:43
  108.4 1.8 %convert_bitcast_fusion = (bf16[1,2,512,128]{3,2,1,0:T(8,128)(2,1)}, f32[2,512,128]{2,1,0:T(8,128)S(1)}) fusion(f32[2,512,128]{2,1,0:T(8,128)} %reduce-scatter.2.cloned.1.call-done, bf16[1,2,512,128]{3,2,1,0:T(8,128)(2,1)S(1)} %copy-done.2), kind=kLoop, calls=%fused_computation.28 | loop fusion | flops 393216 | bytes 1572864 | tf_op jit(solution)/shard_map/broadcast_in_dim | solution.py:48
  110.2 1.9 %fusion.25 = bf16[512,128]{1,0:T(8,128)(2,1)} fusion(f32[2,512,128]{2,1,0:T(8,128)S(1)} %get-tuple-element.4, f32[]{:T(128)} %bitcast.14, f32[]{:T(128)} %bitcast.13), kind=kLoop, calls=%fused_computation.32 | loop fusion | flops 262144 | bytes 655368 | tf_op jit(solution)/shard_map/convert_element_type | solution.py:47
  112.1 0.0 all-reduce.2.cloned.1.call-update
  112.1 31.1 %all-reduce.2.cloned.1.call-done = bf16[512,128]{1,0:T(8,128)(2,1)} async-done(((bf16[512,128]{1,0:T(8,128)(2,1)}), bf16[512,128]{1,0:T(8,128)(2,1)}) %all-reduce.2.cloned.1.call-update) | async-done | bytes 131088 | tf_op jit(solution)/shard_map/psum | solution.py:47
  143.2 1.6 %convert_element_type.32 = f32[512,128]{1,0:T(8,128)} convert(bf16[512,128]{1,0:T(8,128)(2,1)} %all-reduce.2.cloned.1.call-done) | non-fusion elementwise | flops 65536 | bytes 393216 | tf_op jit(solution)/shard_map/convert_element_type | solution.py:47
  (7 shorter events, 0.1 us)
Async XLA Ops:
  7.2 53.8 %all-gather.2.cloned.1.call-start = ((), (), s32[]{:S(2)}) async-start(), calls=%async_computation.2 | async-start | bytes 1966080 | tf_op jit(solution)/shard_map/all_gather | solution.py:33
  9.6 13.9 %copy-start.1 = (bf16[1,2,4,96,192]{4,3,2,1,0:T(8,128)(2,1)S(1)}, bf16[1,2,4,96,192]{4,3,2,1,0:T(8,128)(2,1)}, u32[]{:S(2)}) copy-start(bf16[1,2,4,96,192]{4,3,2,1,0:T(8,128)(2,1)} %param.5) | copy-start | bytes 884740
  23.4 10.7 %copy-start = (bf16[1,2,2,96,512]{4,3,2,1,0:T(8,128)(2,1)S(1)}, bf16[1,2,2,96,512]{4,3,2,1,0:T(8,128)(2,1)}, u32[]{:S(2)}) copy-start(bf16[1,2,2,96,512]{4,3,2,1,0:T(8,128)(2,1)} %copy.14) | copy-start | bytes 1179652
  23.4 84.9 %reduce-scatter.2.cloned.1.call-start = ((), (), s32[]{:S(2)}) async-start(), calls=%async_computation.3 | async-start | bytes 2621440 | tf_op jit(solution)/shard_map/reduce_scatter | solution.py:43
  63.6 2.1 %copy-start.4 = (f32[384,512]{1,0:T(8,128)}, f32[384,512]{1,0:T(8,128)S(1)}, u32[]{:S(2)}) copy-start(f32[384,512]{1,0:T(8,128)S(1)} %fusion.4) | copy-start | bytes 2359300
  65.7 0.7 copy-start.3
  65.7 42.7 %copy-start.2 = (bf16[1,2,512,128]{3,2,1,0:T(8,128)(2,1)S(1)}, bf16[1,2,512,128]{3,2,1,0:T(8,128)(2,1)}, u32[]{:S(2)}) copy-start(bf16[1,2,512,128]{3,2,1,0:T(8,128)(2,1)} %param.8) | copy-start | bytes 786436
  65.7 77.5 %all-reduce.2.cloned.1.call-start = ((), (), s32[]{:S(2)}) async-start(), calls=%async_computation.4 | async-start | bytes 262144 | tf_op jit(solution)/shard_map/psum | solution.py:47
Sparse Core Ops, SparseCore 0:
  23.5 37.4 all-gather.1
  65.8 42.5 reduce-scatter.1
  112.2 30.9 all-reduce.1
where the time goes:
time: 152 us; the launch traced here: 151 us
  waiting for transfers between devices  99.4 us (65%)
  blocking collectives  22.7 us (15%)
  between operations  13.8 us (9%)
  other arithmetic  7.29 us (5%)
  local copies, waits for them, and re-layouts  4.86 us (3%)
  matrix products  3.19 us (2%)
    reduce_scatter x1, waiting for transfers between devices, body(): lax.psum_scatter(diag_terms, 'row', scatter_dimension=2, tiled=True)  41.4 us
    psum x1, waiting for transfers between devices, body(): lax.psum(density_term.astype(jnp.bfloat16), 'pole').astype(jnp.float32)  31.1 us
    all_gather x1, waiting for transfers between devices, body(): full_cols = lax.all_gather(local_rows, 'row', axis=2, tiled=True)  26.8 us
    all_to_all x1, blocking collectives, body(): lax.all_to_all(masked, 'col', split_axis=3, concat_axis=2, tiled=True)  12.2 us
    all_gather x1, blocking collectives, body(): segment = lax.all_gather(anc_inverse, 'col', axis=3, tiled=True)  10.5 us
    dot_general x2, matrix products, complex_left(): lax.dot_general(left_side, right_side, (((0,), (0,)), ((), ())), preferre...  3.19 us
  transfers between devices with their start and end apart: 3, of which 3 were waited for; matrix products, arithmetic and copies ran while one was open for 1% of the time, Pallas kernels for 0%

commit v1 on v0

v1 whole, which is shorter than its diff:
```python
import functools

import jax
import jax.numpy as jnp
from jax import lax
from jax.experimental import pallas as pl
from jax.experimental.pallas import tpu as pltpu
from jax.sharding import PartitionSpec as P

MESH = pl.DeviceIdType.MESH
F32 = jnp.float32
BF16 = jnp.bfloat16


def kernel(
    n_pole, n_row, n_col,
    anc, panel, pattern, diag, weights,
    out_panel, out_diag, out_density,
    buf, gbuf, lhs, psend, pbuf, rhs, dterm, dsend, drecv, xbuf, fsend, frecv,
    s_y, s_up, s_dn, r_ag, s_g, r_g, s_p, r_p, s_d, r_d, s_x, r_x, s_f, r_f,
):
    p, r, c = lax.axis_index("pole"), lax.axis_index("row"), lax.axis_index("col")
    core = lax.rem(p, 2)
    x_me = p // 2
    partner = p + 1 - 2 * core
    n_x = n_pole // 2
    has_up, has_dn = r + 1 < n_row, r > 0
    rows = panel.shape[2]
    width = panel.shape[3] // n_col
    chunk = width // n_row
    i_rows = anc.shape[4]
    n_fine = n_row * n_col
    deep = n_fine * 2 * rows
    order = [0] + list(range(n_row - 1, n_row // 2, -1)) + list(range(1, n_row // 2 + 1))

    def remote(src, dst, send, recv, **where):
        return pltpu.make_async_remote_copy(
            src_ref=src, dst_ref=dst, send_sem=send, recv_sem=recv, device_id=where, device_id_type=MESH
        )

    barrier = pltpu.get_barrier_semaphore()

    def greet(**where):
        pl.semaphore_signal(barrier, inc=1, device_id=where, device_id_type=MESH)

    @pl.when(has_up)
    def _():
        greet(row=r + 1)

    @pl.when(has_dn)
    def _():
        greet(row=r - 1)

    for k in range(1, n_col):
        greet(col=lax.rem(c + k, n_col))
    greet(pole=partner)
    for k in range(1, n_x):
        greet(pole=lax.rem(p + 2 * k, n_pole))
    near = has_up.astype(jnp.int32) + has_dn.astype(jnp.int32)
    pl.semaphore_wait(barrier, near + (n_col - 1) + 1 + (n_x - 1))

    pending = []

    def start(copy, cond=None):
        if cond is None:
            copy.start()
        else:
            pl.when(cond)(copy.start)
        pending.append((copy, cond))

    def cols(col, t):
        return pl.ds(pl.multiple_of(col * width + t * chunk, chunk), chunk)

    def send_y(t):
        for k in range(1, n_col):
            other = lax.rem(c + k, n_col)
            f = r * n_col + c
            start(remote(panel.at[0, :, :, cols(other, t)], buf.at[t, f], s_y.at[t, k - 1], r_ag.at[t, f], col=other))

    def got(t, f):
        piece = buf.at[t, f]
        remote(piece, piece, s_y.at[0, 0], r_ag.at[t, f], col=c).wait_recv()

    def up(t, f, src, cond):
        start(remote(src, buf.at[t, f], s_up.at[t, f], r_ag.at[t, f], row=r + 1), cond)

    def down(t, f, src, cond):
        start(remote(src, buf.at[t, f], s_dn.at[t, f], r_ag.at[t, f], row=r - 1), cond)

    mine = r * n_col + c

    def send_own(t):
        up(t, mine, panel.at[0, :, :, cols(c, t)], has_up)
        down(t, mine, panel.at[0, :, :, cols(c, t)], has_dn)

    def mask(f):
        return pattern[f, c].astype(F32)

    def prepare():
        for k in range(1, n_col):
            f = lax.rem(c + k, n_col)
            remote(anc.at[0], gbuf.at[f], s_g.at[0], r_g.at[f], col=c).wait_recv()
        for q in range(n_row):
            for u in range(0, n_col, 2):
                top, low = [], []
                for v in (u, u + 1):
                    scale = -mask(q * n_col + v)
                    re = gbuf[v, 0, q].astype(F32) * scale
                    im = gbuf[v, 1, q].astype(F32) * scale
                    top += [re, -im]
                    low += [im, re]
                at = (q * n_col + u) * 2 * rows
                lhs[0:i_rows, at:at + 4 * rows] = jnp.concatenate(top, axis=0).T.astype(BF16)
                lhs[i_rows:, at:at + 4 * rows] = jnp.concatenate(low, axis=0).T.astype(BF16)

    def compute(t):
        right = buf[t].reshape(deep, chunk)
        for part in range(2):
            got_part = jnp.dot(lhs[part * i_rows:(part + 1) * i_rows], right, preferred_element_type=F32)
            out_panel[0, part, :, t * chunk:(t + 1) * chunk] = got_part
            rounded = got_part.astype(BF16).astype(F32)
            for v in range(n_col):
                psend[t, v, part] = (rounded[v * rows:(v + 1) * rows] * mask(r * n_col + v)).astype(BF16)

        @pl.when(r == t)
        def _():
            pbuf[t] = psend[t]

        start(remote(psend.at[t], pbuf.at[r], s_p.at[t], r_p.at[r], row=t), r != t)

    send_y(order[0])
    send_own(order[0])
    if n_row > 1:
        send_y(order[1])
    for k in range(1, n_col):
        start(remote(anc.at[0], gbuf.at[c], s_g.at[k - 1], r_g.at[c], col=lax.rem(c + k, n_col)))
    for t in order[2:]:
        send_y(t)
    for t in range(n_row):
        buf[t, mine] = panel[0, :, :, cols(c, t)]
    gbuf[c] = anc[0]

    for s in range(2 * n_row - 1):
        if s < n_row:
            t = order[s]
            if s > 0:
                send_own(t)
            for k in range(1, n_col):
                f = r * n_col + lax.rem(c + k, n_col)
                got(t, f)
                up(t, f, buf.at[t, f], has_up)
                down(t, f, buf.at[t, f], has_dn)
        for d in range(1, n_row):
            if not 0 <= s - d < n_row:
                continue
            t = order[s - d]
            for k in range(n_col):
                v = lax.rem(c + k, n_col)
                below, above = r >= d, r + d < n_row
                f_below, f_above = (r - d) * n_col + v, (r + d) * n_col + v
                pl.when(below)(functools.partial(got, t, f_below))
                up(t, f_below, buf.at[t, f_below], below & has_up)
                pl.when(above)(functools.partial(got, t, f_above))
                down(t, f_above, buf.at[t, f_above], above & has_dn)
        if s == n_row - 2:
            prepare()
        if s >= n_row - 1:
            compute(order[s - n_row + 1])

    for k in range(1, n_row):
        other = lax.rem(r + k, n_row)
        remote(psend.at[0], pbuf.at[other], s_p.at[0], r_p.at[other], row=r).wait_recv()
    for q in range(n_row):
        for v in range(n_col):
            f = q * n_col + v
            re, im = pbuf[q, v, 0], pbuf[q, v, 1]
            rhs[f, 0, :, 0:chunk] = re
            rhs[f, 0, :, chunk:] = im
            rhs[f, 1, :, 0:chunk] = -im
            rhs[f, 1, :, chunk:] = re
    right = rhs[...].reshape(deep, 2 * chunk)
    w_re, w_im = weights[0, 0], weights[0, 1]
    for t in range(n_row):
        part = lax.dot_general(
            buf[t].reshape(deep, chunk), right, (((0,), (0,)), ((), ())), preferred_element_type=F32
        )
        at = slice(t * chunk, (t + 1) * chunk)
        d_re = diag[0, 0, at].astype(F32) - part[:, 0:chunk]
        d_im = diag[0, 1, at].astype(F32) - part[:, chunk:]
        out_diag[0, 0, at] = d_re.astype(BF16)
        out_diag[0, 1, at] = d_im.astype(BF16)
        term = w_re * d_im + w_im * d_re
        dterm[at] = term
        dsend[at] = term.astype(BF16)

    half = width // 2
    keep = pl.ds(pl.multiple_of(core * half, half), half)
    give = pl.ds(pl.multiple_of((1 - core) * half, half), half)
    swap = remote(dsend.at[give], drecv, s_d, r_d, pole=partner)
    start(swap)
    swap.wait_recv()
    xbuf[x_me] = (dterm[keep] + drecv[...].astype(F32)).astype(BF16)
    for k in range(1, n_x):
        start(remote(xbuf.at[x_me], xbuf.at[x_me], s_x.at[k - 1], r_x.at[x_me], pole=lax.rem(p + 2 * k, n_pole)))
    for k in range(1, n_x):
        other = lax.rem(x_me + k, n_x)
        remote(xbuf.at[other], xbuf.at[other], s_x.at[0], r_x.at[other], pole=p).wait_recv()
    total = xbuf[0].astype(F32)
    for k in range(1, n_x):
        total += xbuf[k].astype(F32)
    fsend[...] = total
    back = remote(fsend, frecv, s_f, r_f, pole=partner)
    start(back)
    out_density[keep] = total
    for copy, cond in pending:
        if cond is None:
            copy.wait_send()
        else:
            pl.when(cond)(copy.wait_send)
    back.wait_recv()
    out_density[give] = frecv[...]


def body(anc_inverse, panel, pattern, diag_inverse, pole_weights):
    n_pole, n_row, n_col = lax.axis_size("pole"), lax.axis_size("row"), lax.axis_size("col")
    rows = panel.shape[2]
    width = panel.shape[3] // n_col
    chunk = width // n_row
    i_rows = anc_inverse.shape[4]
    n_fine = n_row * n_col
    deep = n_fine * 2 * rows
    n_x = n_pole // 2
    half = width // 2
    dma = pltpu.SemaphoreType.DMA
    vmem = pl.BlockSpec(memory_space=pltpu.VMEM)
    smem = pl.BlockSpec(memory_space=pltpu.SMEM)
    return pl.pallas_call(
        functools.partial(kernel, n_pole, n_row, n_col),
        out_shape=(
            jax.ShapeDtypeStruct((1, 2, i_rows, width), F32),
            jax.ShapeDtypeStruct(diag_inverse.shape, BF16),
            jax.ShapeDtypeStruct((width, chunk), F32),
        ),
        in_specs=[vmem, vmem, smem, vmem, smem],
        out_specs=(vmem, vmem, vmem),
        scratch_shapes=[
            pltpu.VMEM((n_row, n_fine, 2, rows, chunk), BF16),
            pltpu.VMEM((n_col, 2, n_row, rows, i_rows), BF16),
            pltpu.VMEM((2 * i_rows, deep), BF16),
            pltpu.VMEM((n_row, n_col, 2, i_rows // n_col, chunk), BF16),
            pltpu.VMEM((n_row, n_col, 2, i_rows // n_col, chunk), BF16),
            pltpu.VMEM((n_fine, 2, rows, 2 * chunk), BF16),
            pltpu.VMEM((width, chunk), F32),
            pltpu.VMEM((width, chunk), BF16),
            pltpu.VMEM((half, chunk), BF16),
            pltpu.VMEM((n_x, half, chunk), BF16),
            pltpu.VMEM((half, chunk), F32),
            pltpu.VMEM((half, chunk), F32),
            dma((n_row, n_col - 1)),
            dma((n_row, n_fine)),
            dma((n_row, n_fine)),
            dma((n_row, n_fine)),
            dma((n_col - 1,)),
            dma((n_col,)),
            dma((n_row,)),
            dma((n_row,)),
            dma,
            dma,
            dma((n_x,)),
            dma((n_x,)),
            dma,
            dma,
        ],
        compiler_params=pltpu.CompilerParams(
            collective_id=0, has_side_effects=True, vmem_limit_bytes=67043328
        ),
    )(anc_inverse, panel, pattern, diag_inverse, pole_weights)


def solution(mesh):
    placed = (
        P("pole", None, None, "col", "row"),
        P("pole", None, ("row", "col"), None),
        P(),
        P("pole", None, "col", "row"),
        P("pole", None),
    )
    return jax.shard_map(
        body,
        mesh=mesh,
        in_specs=placed,
        out_specs=(P("pole", None, "row", "col"), P("pole", None, "col", "row"), P("col", "row")),
        check_vma=False,
    )
```

time: 152 us -> 59.8 us (0.39)
  the two profiles are of different devices: /device:TPU:0 before, /device:TPU:17 now
where the time goes in v1:
time: 59.8 us; the launch traced here: 59.5 us
  Pallas kernels  53.7 us (90%)
  local copies, waits for them, and re-layouts  5.2 us (9%)
  between operations  0.65 us (1%)
    pallas_call x1, Pallas kernels, body(): pl.pallas_call(functools.partial(kernel, n_pole, n_row, n_col), out_shape...  53.7 us
    unnamed x8, local copies, waits for them, and re-layouts  5.2 us

profile of v1, /device:TPU:17, one launch (start us, length us, event | category | flops | bytes accessed | tf_op | source)
XLA Modules:
  0.0 59.5 jit_solution(9152761705439809353)
XLA Ops:
  0.6 1.3 %copy.8.pattern = s32[8,2]{1,0:T(8,128)} copy(s32[8,2]{0,1:T(2,128)} %param.7) | data formatting | bytes 128 | tf_op args[2]
  2.0 53.7 %shard_map.76 = (f32[1,2,192,512]{3,2,1,0:T(8,128)}, bf16[1,2,512,128]{3,2,1,0:T(8,128)(2,1)}, f32[512,128]{1,0:T(8,128)}) custom-call(bf16[1,2,4,96,192]{4,3,2,1,0:T(8,128)(2,1)} %anc.1, bf16[1,2,96,1024]{3,2,1,0:T(8,128)(2,1)} %panel.1, s32[8,2]{1,0:T(8,128)} %copy.8.pattern, bf16[1,2,512,128]{3,2,1,0:T(8,128)(2,1)} %diag.1, f32[1,2]{1,0:T(1,128)} %weights.1), custom_call_target="tpu_custom_call" | custom-call | tf_op jit(solution)/shard_map/pallas_call | solution.py:237
  55.7 0.0 copy-start.1
  55.7 2.1 %copy.12 = f32[1,2,192,512]{3,2,1,0:T(8,128)} copy(f32[1,2,192,512]{3,2,1,0:T(8,128)} %get-tuple-element.6) | data formatting | bytes 1572864
  57.8 0.0 copy-done.1
  57.8 0.0 copy-start
  57.8 0.7 %copy.13 = bf16[1,2,512,128]{3,2,1,0:T(8,128)(2,1)} copy(bf16[1,2,512,128]{3,2,1,0:T(8,128)(2,1)S(1)} %copy-done.1) | data formatting | bytes 524288
  58.5 0.3 copy-done
  58.8 0.7 %copy.14 = f32[512,128]{1,0:T(8,128)} copy(f32[512,128]{1,0:T(8,128)S(1)} %copy-done) | data formatting | bytes 524288
Async XLA Ops:
  55.7 2.1 %copy-start.1 = (bf16[1,2,512,128]{3,2,1,0:T(8,128)(2,1)S(1)}, bf16[1,2,512,128]{3,2,1,0:T(8,128)(2,1)}, u32[]{:S(2)}) copy-start(bf16[1,2,512,128]{3,2,1,0:T(8,128)(2,1)} %get-tuple-element.7) | copy-start | bytes 786436
  57.8 1.0 %copy-start = (f32[512,128]{1,0:T(8,128)S(1)}, f32[512,128]{1,0:T(8,128)}, u32[]{:S(2)}) copy-start(f32[512,128]{1,0:T(8,128)} %get-tuple-element.8) | copy-start | bytes 786436
